TPU v7x, 32 devices: a whole 2x2x4 slice. The times are simulated.
32 devices in a mesh: ep: 4 (over z), fsdp: 8 (over y, x, core).
Axes of the slice: x: 2, y: 2, z: 4, core: 2. Of those that a mesh axis runs over, the one named last changes fastest.
Arguments:
- train_gate: float32 [64, 2048, 1408], P('ep', 'fsdp'), may hold values from -0.1875 to 0.1875
- train_up: float32 [64, 2048, 1408], P('ep', 'fsdp'), may hold values from -0.1875 to 0.1875
- train_down: float32 [64, 1408, 2048], P('ep', None, 'fsdp'), may hold values from -0.21875 to 0.21875
- router_weight: float32 [2048, 64], P('fsdp', 'ep'), may hold values from -0.125 to 0.125
- router_gain: float32 [2048], P('fsdp'), may hold values from 0.25 to 1.75
Outputs:
- ready_gate: bfloat16 [64, 2048, 1408], P('ep', None, 'fsdp')
- ready_up: bfloat16 [64, 2048, 1408], P('ep', None, 'fsdp')
- ready_down: bfloat16 [64, 1408, 2048], P('ep', 'fsdp')
- scale_gate: float32 [64, 1408], P('ep', 'fsdp')
- scale_up: float32 [64, 1408], P('ep', 'fsdp')
- scale_down: float32 [64, 1408], P('ep', 'fsdp')
- serve_router: bfloat16 [2048, 64], replicated
All inputs are finite; a program needn't handle non-finite values. Where the computation divides by a largest or mean magnitude, that divisor is 1e-20 or more.
Results may differ from a plain program's by a relative error of at most 0.012.
Values may be sent and summed in bfloat16 or wider, within the bound.
A program may use at most 192 MiB of HBM per device.

v0:
```python
import functools

import jax
import jax.numpy as jnp
from jax import lax
from jax.experimental import pallas as pl
from jax.experimental.pallas import tpu as pltpu
from jax.sharding import PartitionSpec as P

VMEM_LIMIT = 60 * 1024 * 1024


def pack_kernel(turn, x_ref, *refs):
    out_ref = refs[-1]
    block = x_ref[0]
    if turn:
        block = block.T
    out_ref[...] = block.reshape(out_ref.shape).astype(jnp.bfloat16)


def pack(train, turn, first, count, carried, at, slots, peers):
    _, rows, columns = train.shape
    outer, inner = (columns, rows) if turn else (rows, columns)
    share = outer // peers
    hbm = pl.BlockSpec(memory_space=pl.ANY)
    return pl.pallas_call(
        functools.partial(pack_kernel, turn),
        grid=(count,),
        in_specs=[pl.BlockSpec((1, rows, columns), lambda e: (first + e, 0, 0))] + [hbm] * len(carried),
        out_specs=pl.BlockSpec((peers, 1, share, inner), lambda e: (0, at + e, 0, 0)),
        out_shape=jax.ShapeDtypeStruct((peers, slots, share, inner), jnp.bfloat16),
        input_output_aliases={1: 0} if carried else {},
        compiler_params=pltpu.CompilerParams(vmem_limit_bytes=VMEM_LIMIT),
        cost_estimate=pl.CostEstimate(
            flops=count * rows * columns, bytes_accessed=count * rows * columns * 6, transcendentals=0
        ),
    )(train, *carried)


def finish_kernel(width, x_ref, *refs):
    ready_ref, scale_ref = refs[-2:]
    peers, _, share, inner = x_ref.shape
    total = jnp.zeros((share, inner), jnp.float32)
    for p in range(peers):
        total += jnp.abs(x_ref[p, 0].astype(jnp.float32))
    scale = jnp.sum(total, axis=1, keepdims=True) / width
    for p in range(peers):
        ready_ref[0, :, p * inner : (p + 1) * inner] = (
            x_ref[p, 0].astype(jnp.float32) / scale
        ).astype(jnp.bfloat16)
    scale_ref[0] = jnp.broadcast_to(scale, (share, 128)).T[0:1]


def finish(received, at, count, carried, first, experts):
    peers, _, share, inner = received.shape
    width = peers * inner
    hbm = pl.BlockSpec(memory_space=pl.ANY)
    return pl.pallas_call(
        functools.partial(finish_kernel, width),
        grid=(count,),
        in_specs=[pl.BlockSpec((peers, 1, share, inner), lambda e: (0, at + e, 0, 0))] + [hbm] * len(carried),
        out_specs=[
            pl.BlockSpec((1, share, width), lambda e: (first + e, 0, 0)),
            pl.BlockSpec((1, 1, share), lambda e: (first + e, 0, 0)),
        ],
        out_shape=[
            jax.ShapeDtypeStruct((experts, share, width), jnp.bfloat16),
            jax.ShapeDtypeStruct((experts, 1, share), jnp.float32),
        ],
        input_output_aliases={1: 0, 2: 1} if carried else {},
        compiler_params=pltpu.CompilerParams(vmem_limit_bytes=VMEM_LIMIT),
        cost_estimate=pl.CostEstimate(
            flops=count * share * width * 4, bytes_accessed=count * share * width * 4, transcendentals=0
        ),
    )(received, *carried)


def shards(ep, fsdp, train_gate, train_up, train_down, router_weight, router_gain):
    experts = train_gate.shape[0]
    part = (router_weight * router_gain[:, None]).astype(jnp.bfloat16).T
    copies = jnp.broadcast_to(part[None], (ep * fsdp,) + part.shape)
    router = lax.all_to_all(copies, ("ep", "fsdp"), split_axis=0, concat_axis=0, tiled=True)

    edge = max(experts * 5 // 16, 1)
    plan = (
        (("down", 0, edge),),
        (("down", edge, experts - edge), ("gate", 0, experts), ("up", 0, experts - edge)),
        (("up", experts - edge, edge),),
    )
    train = {"gate": train_gate, "up": train_up, "down": train_down}
    done = {"gate": (), "up": (), "down": ()}

    def pack_group(group):
        slots, at, packed = sum(count for _, _, count in group), 0, ()
        for name, first, count in group:
            packed = (pack(train[name], name != "down", first, count, packed, at, slots, fsdp),)
            at += count
        return packed[0]

    def finish_group(group, received):
        at = 0
        for name, first, count in group:
            done[name] = finish(received, at, count, done[name], first, experts)
            at += count

    def exchange(packed):
        return lax.all_to_all(packed, "fsdp", split_axis=0, concat_axis=0, tiled=True)

    packed, router = lax.optimization_barrier((pack_group(plan[0]), router))
    received = exchange(packed)
    for last, group in zip(plan, plan[1:]):
        received, packed, done = lax.optimization_barrier((received, pack_group(group), done))
        arrived, received = received, exchange(packed)
        finish_group(last, arrived)
    received, done = lax.optimization_barrier((received, done))
    finish_group(plan[-1], received)

    router = router.reshape((ep, fsdp) + part.shape).transpose(1, 3, 0, 2)
    serve_router = router.reshape(fsdp * part.shape[1], ep * part.shape[0])
    (ready_gate, scale_gate), (ready_up, scale_up), (ready_down, scale_down) = (
        done["gate"],
        done["up"],
        done["down"],
    )
    return (
        jnp.swapaxes(ready_gate, 1, 2),
        jnp.swapaxes(ready_up, 1, 2),
        ready_down,
        scale_gate[:, 0],
        scale_up[:, 0],
        scale_down[:, 0],
        serve_router,
    )


def solution(mesh):
    in_specs = (
        P("ep", "fsdp", None),
        P("ep", "fsdp", None),
        P("ep", None, "fsdp"),
        P("fsdp", "ep"),
        P("fsdp"),
    )
    out_specs = (
        P("ep", None, "fsdp"),
        P("ep", None, "fsdp"),
        P("ep", "fsdp", None),
        P("ep", "fsdp"),
        P("ep", "fsdp"),
        P("ep", "fsdp"),
        P(),
    )
    body = functools.partial(shards, mesh.shape["ep"], mesh.shape["fsdp"])
    return jax.shard_map(body, mesh=mesh, in_specs=in_specs, out_specs=out_specs, check_vma=False)
```

profile of v0, /device:TPU:0, one launch (start us, length us, event | category | flops | bytes accessed | tf_op | source)
XLA Modules:
  0.0 428.8 jit_solution(5097164724395214162)
XLA Ops:
  0.6 0.7 fusion
  1.4 0.7 broadcast_in_dim.2
  2.1 7.3 %all-to-all-start = ((bf16[32,16,256]{2,1,0:T(8,128)(2,1)}), bf16[32,16,256]{2,1,0:T(8,128)(2,1)S(1)}, u32[]{:S(2)}, u32[]{:S(2)}) async-start(bf16[32,16,256]{2,1,0:T(8,128)(2,1)} %broadcast_in_dim.2), calls=%async_computation | async-start | bytes 524288 | tf_op jit(solution)/shard_map/all_to_all | solution.py:82
  9.4 6.4 %shard_map.108 = bf16[8,5,176,256]{3,2,1,0:T(8,128)(2,1)} custom-call(f32[16,1408,256]{2,1,0:T(8,128)} %x_ref.6), custom_call_target="tpu_custom_call" | custom-call | flops 1802240 | bytes 10813440 | tf_op jit(solution)/shard_map/pallas_call | solution.py:26
  15.8 4.2 all-to-all-done
  20.0 4.5 %all-to-all-start.1 = ((bf16[8,5,176,256]{3,2,1,0:T(8,128)(2,1)}), bf16[8,5,176,256]{3,2,1,0:T(8,128)(2,1)}, u32[]{:S(2)}, u32[]{:S(2)}) async-start(bf16[8,5,176,256]{3,2,1,0:T(8,128)(2,1)} %shard_map.108), calls=%async_computation.1 | async-start | bytes 7208960 | tf_op jit(solution)/shard_map/all_to_all | solution.py:107
  24.5 12.6 %shard_map.109.refs_0_ = bf16[8,38,176,256]{3,2,1,0:T(8,128)(2,1)} custom-call(f32[16,1408,256]{2,1,0:T(8,128)} %x_ref.6), custom_call_target="tpu_custom_call" | custom-call | flops 3964928 | bytes 23789568 | tf_op jit(solution)/shard_map/pallas_call | solution.py:26
  37.1 18.5 %shard_map.110.refs_0_ = bf16[8,38,176,256]{3,2,1,0:T(8,128)(2,1)} custom-call(f32[16,256,1408]{2,1,0:T(8,128)} %x_ref.7, bf16[8,38,176,256]{3,2,1,0:T(8,128)(2,1)} %shard_map.109.refs_0_), custom_call_target="tpu_custom_call", output_to_operand_aliasing={{}: (1, {})} | custom-call | flops 5767168 | bytes 34603008 | tf_op jit(solution)/shard_map/pallas_call | solution.py:26
  55.6 13.6 %shard_map.111 = bf16[8,38,176,256]{3,2,1,0:T(8,128)(2,1)} custom-call(f32[16,256,1408]{2,1,0:T(8,128)} %x_ref.9, bf16[8,38,176,256]{3,2,1,0:T(8,128)(2,1)} %shard_map.110.refs_0_), custom_call_target="tpu_custom_call", output_to_operand_aliasing={{}: (1, {})} | custom-call | flops 3964928 | bytes 23789568 | tf_op jit(solution)/shard_map/pallas_call | solution.py:26
  69.2 0.0 all-to-all-done.1.x_ref
  69.2 6.6 %all-to-all-start.2 = ((bf16[8,38,176,256]{3,2,1,0:T(8,128)(2,1)}), bf16[8,38,176,256]{3,2,1,0:T(8,128)(2,1)}, u32[]{:S(2)}, u32[]{:S(2)}) async-start(bf16[8,38,176,256]{3,2,1,0:T(8,128)(2,1)} %shard_map.111), calls=%async_computation.2 | async-start | bytes 54788096 | tf_op jit(solution)/shard_map/all_to_all | solution.py:107
  75.8 6.9 %shard_map.112 = bf16[8,5,176,256]{3,2,1,0:T(8,128)(2,1)} custom-call(f32[16,256,1408]{2,1,0:T(8,128)} %x_ref.9), custom_call_target="tpu_custom_call" | custom-call | flops 1802240 | bytes 10813440 | tf_op jit(solution)/shard_map/pallas_call | solution.py:26
  82.7 6.1 %shard_map.113 = (bf16[16,176,2048]{2,1,0:T(8,128)(2,1)}, f32[16,1,176]{2,1,0:T(1,128)}) custom-call(bf16[8,5,176,256]{3,2,1,0:T(8,128)(2,1)} %all-to-all-done.1.x_ref), custom_call_target="tpu_custom_call" | custom-call | flops 7208960 | bytes 7208960 | tf_op jit(solution)/shard_map/pallas_call | solution.py:58
  88.8 284.6 %all-to-all-done.2.x_ref = bf16[8,38,176,256]{3,2,1,0:T(8,128)(2,1)} async-done(((bf16[8,38,176,256]{3,2,1,0:T(8,128)(2,1)}), bf16[8,38,176,256]{3,2,1,0:T(8,128)(2,1)}, u32[]{:S(2)}, u32[]{:S(2)}) %all-to-all-start.2) | async-done | bytes 27394080 | tf_op jit(solution)/shard_map/all_to_all | solution.py:107
  373.4 4.5 %all-to-all-start.3 = ((bf16[8,5,176,256]{3,2,1,0:T(8,128)(2,1)}), bf16[8,5,176,256]{3,2,1,0:T(8,128)(2,1)}, u32[]{:S(2)}, u32[]{:S(2)}) async-start(bf16[8,5,176,256]{3,2,1,0:T(8,128)(2,1)} %shard_map.112), calls=%async_computation.3 | async-start | bytes 7208960 | tf_op jit(solution)/shard_map/all_to_all | solution.py:107
  377.9 0.1 copy.18
  378.0 0.8 copy.22
  378.8 12.0 %shard_map.116 = (bf16[16,176,2048]{2,1,0:T(8,128)(2,1)}, f32[16,1,176]{2,1,0:T(1,128)}) custom-call(bf16[8,38,176,256]{3,2,1,0:T(8,128)(2,1)} %all-to-all-done.2.x_ref), custom_call_target="tpu_custom_call" | custom-call | flops 15859712 | bytes 15859712 | tf_op jit(solution)/shard_map/pallas_call | solution.py:58
  390.7 12.0 %shard_map.114 = (bf16[16,176,2048]{2,1,0:T(8,128)(2,1)}, f32[16,1,176]{2,1,0:T(1,128)}) custom-call(bf16[8,38,176,256]{3,2,1,0:T(8,128)(2,1)} %all-to-all-done.2.x_ref, bf16[16,176,2048]{2,1,0:T(8,128)(2,1)} %get-tuple-element.39.refs_0_, f32[16,1,176]{2,1,0:T(1,128)} %get-tuple-element.40.refs_1_), custom_call_target="tpu_custom_call", output_to_operand_aliasing={{0}: (1, {}), {1}: (2, {})} | custom-call | flops 15859712 | bytes 15859712 | tf_op jit(solution)/shard_map/pallas_call | solution.py:58
  402.7 16.2 %shard_map.115 = (bf16[16,176,2048]{2,1,0:T(8,128)(2,1)}, f32[16,1,176]{2,1,0:T(1,128)}) custom-call(bf16[8,38,176,256]{3,2,1,0:T(8,128)(2,1)} %all-to-all-done.2.x_ref), custom_call_target="tpu_custom_call" | custom-call | flops 23068672 | bytes 23068672 | tf_op jit(solution)/shard_map/pallas_call | solution.py:58
  418.9 0.0 copy-start
  418.9 0.0 copy-start.1
  418.9 1.8 all-to-all-done.3.x_ref
  420.7 6.1 %shard_map.117 = (bf16[16,176,2048]{2,1,0:T(8,128)(2,1)}, f32[16,1,176]{2,1,0:T(1,128)}) custom-call(bf16[8,5,176,256]{3,2,1,0:T(8,128)(2,1)} %all-to-all-done.3.x_ref, bf16[16,176,2048]{2,1,0:T(8,128)(2,1)} %get-tuple-element.49.refs_0_, f32[16,1,176]{2,1,0:T(1,128)} %get-tuple-element.50.refs_1_), custom_call_target="tpu_custom_call", output_to_operand_aliasing={{0}: (1, {}), {1}: (2, {})} | custom-call | flops 7208960 | bytes 7208960 | tf_op jit(solution)/shard_map/pallas_call | solution.py:58
  426.9 1.3 copy.26
  428.2 0.0 copy-done
  428.2 0.0 copy-done.1
  428.2 0.6 copy_bitcast_fusion
Async XLA Ops:
  2.1 17.9 %all-to-all-start = ((bf16[32,16,256]{2,1,0:T(8,128)(2,1)}), bf16[32,16,256]{2,1,0:T(8,128)(2,1)S(1)}, u32[]{:S(2)}, u32[]{:S(2)}) async-start(bf16[32,16,256]{2,1,0:T(8,128)(2,1)} %broadcast_in_dim.2), calls=%async_computation | async-start | bytes 524288 | tf_op jit(solution)/shard_map/all_to_all | solution.py:82
  20.0 49.2 %all-to-all-start.1 = ((bf16[8,5,176,256]{3,2,1,0:T(8,128)(2,1)}), bf16[8,5,176,256]{3,2,1,0:T(8,128)(2,1)}, u32[]{:S(2)}, u32[]{:S(2)}) async-start(bf16[8,5,176,256]{3,2,1,0:T(8,128)(2,1)} %shard_map.108), calls=%async_computation.1 | async-start | bytes 7208960 | tf_op jit(solution)/shard_map/all_to_all | solution.py:107
  69.2 304.3 %all-to-all-start.2 = ((bf16[8,38,176,256]{3,2,1,0:T(8,128)(2,1)}), bf16[8,38,176,256]{3,2,1,0:T(8,128)(2,1)}, u32[]{:S(2)}, u32[]{:S(2)}) async-start(bf16[8,38,176,256]{3,2,1,0:T(8,128)(2,1)} %shard_map.111), calls=%async_computation.2 | async-start | bytes 54788096 | tf_op jit(solution)/shard_map/all_to_all | solution.py:107
  373.4 47.3 %all-to-all-start.3 = ((bf16[8,5,176,256]{3,2,1,0:T(8,128)(2,1)}), bf16[8,5,176,256]{3,2,1,0:T(8,128)(2,1)}, u32[]{:S(2)}, u32[]{:S(2)}) async-start(bf16[8,5,176,256]{3,2,1,0:T(8,128)(2,1)} %shard_map.112), calls=%async_computation.3 | async-start | bytes 7208960 | tf_op jit(solution)/shard_map/all_to_all | solution.py:107
  418.9 9.3 %copy-start = (f32[16,1,176]{2,1,0:T(1,128)S(1)}, f32[16,1,176]{2,1,0:T(1,128)}, u32[]{:S(2)}) copy-start(f32[16,1,176]{2,1,0:T(1,128)} %get-tuple-element.55) | copy-start | bytes 33796
  418.9 9.3 %copy-start.1 = (f32[16,1,176]{2,1,0:T(1,128)S(1)}, f32[16,1,176]{2,1,0:T(1,128)}, u32[]{:S(2)}) copy-start(f32[16,1,176]{2,1,0:T(1,128)} %get-tuple-element.53) | copy-start | bytes 33796
where the time goes:
time: 432 us; the launch traced here: 429 us
  waiting for transfers between devices  291 us (67%)
  Pallas kernels  110 us (25%)
  starting transfers between devices  22.9 us (5%)
    all_to_all x3, waiting for transfers between devices, exchange(): lax.all_to_all(packed, 'fsdp', split_axis=0, concat_axis=0, tiled=True)  286 us
    pallas_call x5, Pallas kernels, pack(): pl.pallas_call(functools.partial(pack_kernel, turn), grid=(count,), in_sp...  58 us
    pallas_call x5, Pallas kernels, finish(): pl.pallas_call(functools.partial(finish_kernel, width), grid=(count,), in...  52.4 us
    all_to_all x3, starting transfers between devices, exchange(): lax.all_to_all(packed, 'fsdp', split_axis=0, concat_axis=0, tiled=True)  15.6 us
  transfers between devices with their start and end apart: 4, of which 3 were waited for; matrix products, arithmetic and copies ran while one was open for 0% of the time, Pallas kernels for 24%

commit v1 on v0

v1 whole, which is shorter than its diff:
```python
import functools

import jax
import jax.numpy as jnp
from jax import lax
from jax.experimental import pallas as pl
from jax.experimental.pallas import tpu as pltpu
from jax.sharding import PartitionSpec as P

VMEM_LIMIT = 60 * 1024 * 1024
FINISH_LIMIT = 24 * 1024 * 1024
TILE = 16
DEPTH = 4
MESH = pl.DeviceIdType.MESH
RING = 6


def ship_kernel(
    sizes, keep, down_ref, gate_ref, up_ref, router_ref, gain_ref,
    received_ref, packed_ref, copies_ref,
    down_in, gate_in, up_in, ring, column,
    load_sem, send_sem, recv_sem, router_sem,
):
    ep, fsdp = sizes
    row, me = lax.axis_index("ep"), lax.axis_index("fsdp")
    experts = down_ref.shape[0]
    sources = ((down_ref, down_in), (gate_ref, gate_in), (up_ref, up_in))

    def load(e, kind):
        source, held = sources[kind]
        slot = lax.rem(e, 2)
        return pltpu.make_async_copy(source.at[e], held.at[slot], load_sem.at[slot, kind])

    def pack(e, kind):
        block = sources[kind][1][lax.rem(e, 2)].astype(jnp.bfloat16)
        if kind:
            block = block.T
        ring[lax.rem(e, RING), kind] = block.reshape(ring.shape[2:])

    def sent(e, kind):
        at = ring.at[lax.rem(e, RING), kind]
        return pltpu.make_async_copy(at, received_ref.at[:, 0, kind], send_sem.at[lax.rem(e, RING), kind])

    def send(e, kind):
        slot = lax.rem(e, RING)
        for step in range(1, fsdp):
            peer = lax.rem(me + step, fsdp)
            pltpu.make_async_remote_copy(
                src_ref=ring.at[slot, kind, peer],
                dst_ref=received_ref.at[me, e, kind],
                send_sem=send_sem.at[slot, kind],
                recv_sem=recv_sem.at[e],
                device_id={"fsdp": peer},
                device_id_type=MESH,
            ).start()
        pltpu.make_async_copy(
            ring.at[slot, kind, me], received_ref.at[me, e, kind], send_sem.at[slot, kind]
        ).start()

    for e in range(min(2, experts)):
        for kind in range(3):
            load(e, kind).start()

    barrier = pltpu.get_barrier_semaphore()
    for step in range(1, fsdp):
        pl.semaphore_signal(barrier, device_id={"fsdp": lax.rem(me + step, fsdp)}, device_id_type=MESH)
    for step in range(1, ep):
        pl.semaphore_signal(barrier, device_id={"ep": lax.rem(row + step, ep)}, device_id_type=MESH)
    column[row] = (router_ref[...] * gain_ref[...]).astype(jnp.bfloat16)
    pl.semaphore_wait(barrier, fsdp + ep - 2)

    def step_of(e, carry):
        for kind in range(3):
            load(e, kind).wait()

            @pl.when(e >= RING)
            def _():
                sent(e - RING, kind).wait()

            pack(e, kind)

            @pl.when(e + 2 < experts)
            def _():
                load(e + 2, kind).start()

            @pl.when(e < keep)
            def _():
                send(e, kind)

            @pl.when(e >= keep)
            def _():
                slot = lax.rem(e, RING)
                pltpu.make_async_copy(
                    ring.at[slot, kind], packed_ref.at[:, e - keep, kind], send_sem.at[slot, kind]
                ).start()

        return carry

    first = min(RING, keep)
    lax.fori_loop(0, first, step_of, 0)

    def share_row(step):
        return pltpu.make_async_remote_copy(
            src_ref=column.at[row],
            dst_ref=column.at[row],
            send_sem=router_sem.at[0],
            recv_sem=router_sem.at[1],
            device_id={"ep": lax.rem(row + step, ep)},
            device_id_type=MESH,
        )

    def block_of(index):
        width = column.shape[2]
        return copies_ref.at[:, :, pl.ds(pl.multiple_of(index * width, width), width)]

    def share_column(step):
        return pltpu.make_async_remote_copy(
            src_ref=column,
            dst_ref=block_of(me),
            send_sem=router_sem.at[2],
            recv_sem=router_sem.at[3],
            device_id={"fsdp": lax.rem(me + step, fsdp)},
            device_id_type=MESH,
        )

    for step in range(1, ep):
        share_row(step).start()
    lax.fori_loop(first, experts, step_of, 0)
    rows = column.at[pl.ds(0, ep - 1)]
    pltpu.make_async_copy(rows, rows, router_sem.at[0]).wait()
    pltpu.make_async_copy(rows, rows, router_sem.at[1]).wait()
    for step in range(1, fsdp):
        share_column(step).start()
    own = pltpu.make_async_copy(column, block_of(me), router_sem.at[4])
    own.start()

    def settle(e, carry):
        for kind in range(3):
            sent(e, kind).wait()
        return carry

    lax.fori_loop(max(experts - RING, 0), experts, settle, 0)

    def arrive(e, carry):
        blocks = received_ref.at[pl.ds(0, fsdp - 1), e]
        pltpu.make_async_copy(blocks, blocks, recv_sem.at[e]).wait()
        return carry

    lax.fori_loop(0, keep, arrive, 0)
    width = column.shape[2]
    others = copies_ref.at[:, :, pl.ds(0, (fsdp - 1) * width)]
    pltpu.make_async_copy(others, others, router_sem.at[2]).wait()
    pltpu.make_async_copy(others, others, router_sem.at[3]).wait()
    own.wait()


def ship(ep, fsdp, keep, down, gate, up, router, gain):
    experts, rows, columns = gate.shape
    share = columns // fsdp
    last = experts - keep
    hbm = pl.BlockSpec(memory_space=pl.ANY)
    vmem = pl.BlockSpec(memory_space=pltpu.VMEM)
    return pl.pallas_call(
        functools.partial(ship_kernel, (ep, fsdp), keep),
        in_specs=[hbm, hbm, hbm, vmem, vmem],
        out_specs=[hbm, hbm, hbm],
        out_shape=[
            jax.ShapeDtypeStruct((fsdp, keep, 3, share, rows), jnp.bfloat16),
            jax.ShapeDtypeStruct((fsdp, last, 3, share, rows), jnp.bfloat16),
            jax.ShapeDtypeStruct((ep, router.shape[0], fsdp * router.shape[1]), jnp.bfloat16),
        ],
        scratch_shapes=[
            pltpu.VMEM((2, columns, rows), jnp.float32),
            pltpu.VMEM((2, rows, columns), jnp.float32),
            pltpu.VMEM((2, rows, columns), jnp.float32),
            pltpu.VMEM((RING, 3, fsdp, share, rows), jnp.bfloat16),
            pltpu.VMEM((ep,) + router.shape, jnp.bfloat16),
            pltpu.SemaphoreType.DMA((2, 3)),
            pltpu.SemaphoreType.DMA((RING, 3)),
            pltpu.SemaphoreType.DMA((keep,)),
            pltpu.SemaphoreType.DMA((5,)),
        ],
        compiler_params=pltpu.CompilerParams(
            collective_id=0, has_side_effects=True, vmem_limit_bytes=VMEM_LIMIT
        ),
        cost_estimate=pl.CostEstimate(
            flops=experts * rows * columns * 30, bytes_accessed=experts * rows * columns * 18, transcendentals=0
        ),
    )(down, gate, up, router, gain)


def rescale(blocks, width, ready, scale_ref, e):
    peers, share, inner = blocks.shape
    columns = []
    for r in range(0, share, TILE):
        rows = slice(r, min(r + TILE, share))
        parts = [blocks[p, rows].astype(jnp.float32) for p in range(peers)]
        total = sum(jnp.abs(part) for part in parts)
        scale = jnp.sum(total, axis=1, keepdims=True) / width
        inverse = 1.0 / scale
        for p, part in enumerate(parts):
            ready[rows, p * inner : (p + 1) * inner] = (part * inverse).astype(jnp.bfloat16)
        columns.append(scale)
    column = jnp.concatenate(columns, axis=0)
    scale_ref[pl.ds(e, 1), :] = jnp.broadcast_to(column, (share, 128)).T[0:1]


def finish_kernel(x_ref, copies_ref, *refs):
    readies, scales, router_ref = refs[:3], refs[3:6], refs[6]
    held, ready, router, load_sem, store_sem, router_sem = refs[7:]
    peers, count, _, share, inner = x_ref.shape

    def load(e):
        slot = lax.rem(e, DEPTH)
        return pltpu.make_async_copy(x_ref.at[:, e], held.at[slot], load_sem.at[slot])

    def store(e, kind):
        slot = lax.rem(e, DEPTH)
        return pltpu.make_async_copy(ready.at[slot, kind], readies[kind].at[e], store_sem.at[slot, kind])

    for e in range(min(DEPTH, count)):
        load(e).start()
    enter = pltpu.make_async_copy(copies_ref, router, router_sem.at[0])
    leave = pltpu.make_async_copy(router, router_ref, router_sem.at[1])
    enter.start()

    def step_of(e, carry):
        slot = lax.rem(e, DEPTH)
        load(e).wait()
        for kind in range(3):

            @pl.when(e >= DEPTH)
            def _():
                store(e - DEPTH, kind).wait()

            rescale(held.at[slot, :, kind], peers * inner, ready.at[slot, kind], scales[kind], e)
            store(e, kind).start()

        @pl.when(e + DEPTH < count)
        def _():
            load(e + DEPTH).start()

        return carry

    lax.fori_loop(0, count, step_of, 0)
    enter.wait()
    leave.start()

    def settle(e, carry):
        for kind in range(3):
            store(e, kind).wait()
        return carry

    lax.fori_loop(max(count - DEPTH, 0), count, settle, 0)
    leave.wait()


def finish(received, copies, experts):
    peers, count, _, share, inner = received.shape
    width = peers * inner
    hbm = pl.BlockSpec(memory_space=pl.ANY)
    vmem = pl.BlockSpec(memory_space=pltpu.VMEM)
    return pl.pallas_call(
        finish_kernel,
        in_specs=[hbm, hbm],
        out_specs=[hbm] * 3 + [vmem] * 3 + [hbm],
        out_shape=[jax.ShapeDtypeStruct((experts, share, width), jnp.bfloat16)] * 3
        + [jax.ShapeDtypeStruct((experts, share), jnp.float32)] * 3
        + [jax.ShapeDtypeStruct(copies.shape, jnp.bfloat16)],
        scratch_shapes=[
            pltpu.VMEM((DEPTH, peers, 3, share, inner), jnp.bfloat16),
            pltpu.VMEM((DEPTH, 3, share, width), jnp.bfloat16),
            pltpu.VMEM(copies.shape, jnp.bfloat16),
            pltpu.SemaphoreType.DMA((DEPTH,)),
            pltpu.SemaphoreType.DMA((DEPTH, 3)),
            pltpu.SemaphoreType.DMA((2,)),
        ],
        compiler_params=pltpu.CompilerParams(vmem_limit_bytes=VMEM_LIMIT - 8 * 1024 * 1024),
        cost_estimate=pl.CostEstimate(
            flops=count * share * width * 12, bytes_accessed=count * share * width * 12, transcendentals=0
        ),
    )(received, copies)


def close_kernel(first, x_ref, *refs):
    before, readies, scales = refs[3:6], refs[6:9], refs[9:12]
    ready, store_sem = refs[12:]
    peers, count, _, share, inner = x_ref.shape
    for old, new in zip(before, scales):
        new[...] = old[...]
    stores = []
    for e in range(count):
        for kind in range(3):
            rescale(x_ref.at[:, e, kind], peers * inner, ready.at[e, kind], scales[kind], first + e)
            store = pltpu.make_async_copy(ready.at[e, kind], readies[kind].at[first + e], store_sem.at[e, kind])
            store.start()
            stores.append(store)
    for store in stores:
        store.wait()


def close(received, first, carried):
    peers, count, _, share, inner = received.shape
    width = peers * inner
    hbm = pl.BlockSpec(memory_space=pl.ANY)
    vmem = pl.BlockSpec(memory_space=pltpu.VMEM)
    return pl.pallas_call(
        functools.partial(close_kernel, first),
        in_specs=[vmem] + [hbm] * 3 + [vmem] * 3,
        out_specs=[hbm] * 3 + [vmem] * 3,
        out_shape=[jax.ShapeDtypeStruct(old.shape, old.dtype) for old in carried],
        input_output_aliases={1: 0, 2: 1, 3: 2},
        scratch_shapes=[
            pltpu.VMEM((count, 3, share, width), jnp.bfloat16),
            pltpu.SemaphoreType.DMA((count, 3)),
        ],
        compiler_params=pltpu.CompilerParams(vmem_limit_bytes=FINISH_LIMIT),
        cost_estimate=pl.CostEstimate(
            flops=count * share * width * 12, bytes_accessed=count * share * width * 12, transcendentals=0
        ),
    )(received, *carried)


def shards(ep, fsdp, train_gate, train_up, train_down, router_weight, router_gain):
    experts = train_gate.shape[0]
    last = max(experts // 16, 1)
    keep = experts - last
    received, packed, copies = ship(
        ep, fsdp, keep, train_down, train_gate, train_up, router_weight.T, router_gain[None]
    )
    rest = lax.all_to_all(packed, "fsdp", split_axis=0, concat_axis=0, tiled=True)
    *done, copies = finish(received, copies, experts)
    ready_down, ready_gate, ready_up, scale_down, scale_gate, scale_up = close(rest, keep, done)
    serve_router = copies.reshape(-1, copies.shape[2]).T
    return (
        jnp.swapaxes(ready_gate, 1, 2),
        jnp.swapaxes(ready_up, 1, 2),
        ready_down,
        scale_gate,
        scale_up,
        scale_down,
        serve_router,
    )


def solution(mesh):
    in_specs = (
        P("ep", "fsdp", None),
        P("ep", "fsdp", None),
        P("ep", None, "fsdp"),
        P("fsdp", "ep"),
        P("fsdp"),
    )
    out_specs = (
        P("ep", None, "fsdp"),
        P("ep", None, "fsdp"),
        P("ep", "fsdp", None),
        P("ep", "fsdp"),
        P("ep", "fsdp"),
        P("ep", "fsdp"),
        P(),
    )
    body = functools.partial(shards, mesh.shape["ep"], mesh.shape["fsdp"])
    return jax.shard_map(body, mesh=mesh, in_specs=in_specs, out_specs=out_specs, check_vma=False)
```

time: 432 us -> 395 us (0.914)
  waiting for transfers between devices: 291 us -> 4.27 us
  Pallas kernels: 110 us -> 385 us
  starting transfers between devices: 22.9 us -> 3.62 us
    all_to_all x4 -> x1, waiting for transfers between devices: 291 us -> 4.27 us  [shards(): lax.all_to_all(packed, 'fsdp', split_axis=0, concat_axis=0, tiled=True)]
    pallas_call x10 -> x3, Pallas kernels: 110 us -> 385 us  [the longest x1 361 us: ship(): pl.pallas_call(functools.partial(ship_kernel, (ep, fsdp), keep), in_specs...]
    all_to_all x4 -> x1, starting transfers between devices: 22.9 us -> 3.62 us  [shards(): lax.all_to_all(packed, 'fsdp', split_axis=0, concat_axis=0, tiled=True)]
  transfers between devices with their start and end apart: 4 -> 1, of which waited for: 3 -> 1; matrix products, arithmetic and copies ran while one was open for 0% -> 0% of each run, Pallas kernels for 24% -> 6%
where the time goes in v1:
time: 395 us
  Pallas kernels  385 us (97%)
  waiting for transfers between devices  4.27 us (1%)
    pallas_call x1, Pallas kernels, ship(): pl.pallas_call(functools.partial(ship_kernel, (ep, fsdp), keep), in_specs...  361 us
    pallas_call x1, Pallas kernels, finish(): pl.pallas_call(finish_kernel, in_specs=[hbm, hbm], out_specs=[hbm] * 3 +...  22 us
  transfers between devices with their start and end apart: 1, of which 1 were waited for; matrix products, arithmetic and copies ran while one was open for 0% of the time, Pallas kernels for 6%

profile of v1, /device:TPU:0, one launch (start us, length us, event | category | flops | bytes accessed | tf_op | source)
XLA Modules:
  0.0 394.6 jit_solution(12544722315686489214)
XLA Ops:
  0.6 360.6 %shard_map.108 = (bf16[8,15,3,176,256]{4,3,2,1,0:T(8,128)(2,1)}, bf16[8,1,3,176,256]{4,3,2,1,0:T(8,128)(2,1)}, bf16[4,16,2048]{2,1,0:T(8,128)(2,1)}) custom-call(f32[16,1408,256]{2,1,0:T(8,128)} %down_ref.1, f32[16,256,1408]{2,1,0:T(8,128)} %gate_ref.1, f32[16,256,1408]{2,1,0:T(8,128)} %up_ref.1, f32[16,256]{1,0:T(8,128)} %bitcast.9, f32[1,256]{1,0:T(1,128)} %bitcast.10), custom_call_target="tpu_custom_call" | custom-call | flops 173015040 | bytes 103809024 | tf_op jit(solution)/shard_map/pallas_call | solution.py:163
  361.2 3.6 all-to-all-start
  364.8 0.0 copy-start
  364.8 0.9 copy-done
  365.8 22.0 %shard_map.109 = (bf16[16,176,2048]{2,1,0:T(8,128)(2,1)}, bf16[16,176,2048]{2,1,0:T(8,128)(2,1)}, bf16[16,176,2048]{2,1,0:T(8,128)(2,1)}, f32[16,176]{1,0:T(8,12...) custom-call(bf16[8,15,3,176,256]{4,3,2,1,0:T(8,128)(2,1)} %get-tuple-element.24.x_ref, ...), custom_call_target="tpu_custom_call" | custom-call | flops 64880640 | bytes 64880640 | tf_op jit(solution)/shard_map/pallas_call | solution.py:263
  387.8 4.3 %all-to-all-done.x_ref = bf16[8,1,3,176,256]{4,3,2,1,0:T(8,128)(2,1)S(1)} async-done(((bf16[8,1,3,176,256]{4,3,2,1,0:T(8,128)(2,1)}), bf16[8,1,3,176,256]{4,3,2,1,0:T(8,128)(2,1)S(1)}, u32[]{:S(2)}, u32[]{:S(2)}) %all-to-all-start) | async-done | bytes 2162720 | tf_op jit(solution)/shard_map/all_to_all | solution.py:331
  392.1 2.5 shard_map.110
Async XLA Ops:
  361.2 30.9 %all-to-all-start = ((bf16[8,1,3,176,256]{4,3,2,1,0:T(8,128)(2,1)}), bf16[8,1,3,176,256]{4,3,2,1,0:T(8,128)(2,1)S(1)}, u32[]{:S(2)}, u32[]{:S(2)}) async-start(bf16[8,1,3,176,256]{4,3,2,1,0:T(8,128)(2,1)} %get-tuple-element.23), calls=%async_computation | async-start | bytes 4325376 | tf_op jit(solution)/shard_map/all_to_all | solution.py:331
  364.8 1.0 copy-start

commit v2 on v1

v2 whole, which is shorter than its diff:
```python
import functools

import jax
import jax.numpy as jnp
from jax import lax
from jax.experimental import pallas as pl
from jax.experimental.pallas import tpu as pltpu
from jax.sharding import PartitionSpec as P

VMEM_LIMIT = 60 * 1024 * 1024
FINISH_LIMIT = 24 * 1024 * 1024
TILE = 16
DEPTH = 6
MESH = pl.DeviceIdType.MESH
RING = 6


def ship_kernel(
    sizes, keep, down_ref, gate_ref, up_ref, router_ref, gain_ref,
    received_ref, packed_ref, copies_ref,
    down_in, gate_in, up_in, ring, weight, gain, strip,
    load_sem, send_sem, recv_sem, piece_sem, router_sem,
):
    ep, fsdp = sizes
    row, me = lax.axis_index("ep"), lax.axis_index("fsdp")
    experts = down_ref.shape[0]
    sources = ((down_ref, down_in), (gate_ref, gate_in), (up_ref, up_in))

    def load(e, kind):
        source, held = sources[kind]
        slot = lax.rem(e, 2)
        return pltpu.make_async_copy(source.at[e], held.at[slot], load_sem.at[slot, kind])

    def pack(e, kind):
        block = sources[kind][1][lax.rem(e, 2)].astype(jnp.bfloat16)
        if kind:
            block = block.T
        ring[lax.rem(e, RING), :, kind] = block.reshape(fsdp, *ring.shape[3:])

    def sent(e):
        slot = lax.rem(e, RING)
        return pltpu.make_async_copy(ring.at[slot], received_ref.at[:, 0], send_sem.at[slot])

    order = [lax.rem(me + step, fsdp) for step in range(1, fsdp + 1)]

    def ship(src, dst, slot, e, peer):
        return pltpu.make_async_remote_copy(
            src_ref=src,
            dst_ref=dst,
            send_sem=send_sem.at[slot],
            recv_sem=recv_sem.at[e],
            device_id={"fsdp": peer},
            device_id_type=MESH,
        )

    def send(e):
        slot = lax.rem(e, RING)
        for peer in order[:-1]:
            ship(ring.at[slot, peer], received_ref.at[me, e], slot, e, peer).start()
        pltpu.make_async_copy(ring.at[slot, me], received_ref.at[me, e], send_sem.at[slot]).start()

    def piece(at, p):
        share = ring.shape[3]
        rows = pl.ds(pl.multiple_of(p * share, share), share)
        return pltpu.make_async_copy(down_ref.at[0, rows], down_in.at[0, rows], piece_sem.at[at])

    for at, p in enumerate(order):
        piece(at, p).start()
    router = [
        pltpu.make_async_copy(src, dst, router_sem.at[at])
        for at, (src, dst) in enumerate(((router_ref, weight), (gain_ref, gain)))
    ]
    for kind in (1, 2):
        load(0, kind).start()
    for copy in router:
        copy.start()
    for kind in range(3):
        load(1, kind).start()

    barrier = pltpu.get_barrier_semaphore()
    for step in range(1, fsdp):
        pl.semaphore_signal(barrier, device_id={"fsdp": lax.rem(me + step, fsdp)}, device_id_type=MESH)
    for step in range(1, ep):
        pl.semaphore_signal(barrier, device_id={"ep": lax.rem(row + step, ep)}, device_id_type=MESH)
    pl.semaphore_wait(barrier, fsdp + ep - 2)

    for at, p in enumerate(order):
        piece(at, p).wait()
        share = ring.shape[3]
        rows = pl.ds(pl.multiple_of(p * share, share), share)
        ring[0, p, 0] = down_in[0, rows].astype(jnp.bfloat16)
        if at < fsdp - 1:
            ship(ring.at[0, p, 0], received_ref.at[me, 0, 0], 0, 0, p).start()
    for kind in (1, 2):
        load(0, kind).wait()
        pack(0, kind)
        for peer in order[:-1]:
            ship(ring.at[0, peer, kind], received_ref.at[me, 0, kind], 0, 0, peer).start()
    pltpu.make_async_copy(ring.at[0, me], received_ref.at[me, 0], send_sem.at[0]).start()
    if experts > 2:
        for kind in range(3):
            load(2, kind).start()

    def step_of(e, carry):
        for kind in range(3):
            load(e, kind).wait()
            if kind == 0:

                @pl.when(e >= RING)
                def _():
                    sent(e - RING).wait()

            pack(e, kind)

            @pl.when(e + 2 < experts)
            def _():
                load(e + 2, kind).start()

        @pl.when(e < keep)
        def _():
            send(e)

        @pl.when(e >= keep)
        def _():
            slot = lax.rem(e, RING)
            pltpu.make_async_copy(ring.at[slot], packed_ref.at[:, e - keep], send_sem.at[slot]).start()

        return carry

    first = min(RING, keep)
    lax.fori_loop(1, first, step_of, 0)

    width = weight.shape[1]
    mine = strip.at[:, pl.ds(pl.multiple_of(me * width, width), width)]
    for copy in router:
        copy.wait()
    mine[...] = (weight[...] * gain[...]).astype(jnp.bfloat16)
    for peer in order[:-1]:
        pltpu.make_async_remote_copy(
            src_ref=mine,
            dst_ref=mine,
            send_sem=router_sem.at[2],
            recv_sem=router_sem.at[3],
            device_id={"fsdp": peer},
            device_id_type=MESH,
        ).start()
    lax.fori_loop(first, keep, step_of, 0)
    others = strip.at[:, pl.ds(0, (fsdp - 1) * width)]
    pltpu.make_async_copy(others, others, router_sem.at[2]).wait()
    pltpu.make_async_copy(others, others, router_sem.at[3]).wait()
    for step in range(1, ep):
        pltpu.make_async_remote_copy(
            src_ref=strip,
            dst_ref=copies_ref.at[row],
            send_sem=router_sem.at[4],
            recv_sem=router_sem.at[5],
            device_id={"ep": lax.rem(row + step, ep)},
            device_id_type=MESH,
        ).start()
    own = pltpu.make_async_copy(strip, copies_ref.at[row], router_sem.at[6])
    own.start()
    lax.fori_loop(keep, experts, step_of, 0)

    def settle(e, carry):
        sent(e).wait()
        return carry

    lax.fori_loop(max(experts - RING, 0), experts, settle, 0)

    def arrive(e, carry):
        blocks = received_ref.at[pl.ds(0, fsdp - 1), e]
        pltpu.make_async_copy(blocks, blocks, recv_sem.at[e]).wait()
        return carry

    lax.fori_loop(0, keep, arrive, 0)
    others = copies_ref.at[pl.ds(0, ep - 1)]
    pltpu.make_async_copy(others, others, router_sem.at[4]).wait()
    pltpu.make_async_copy(others, others, router_sem.at[5]).wait()
    own.wait()


def ship(ep, fsdp, keep, down, gate, up, router, gain):
    experts, rows, columns = gate.shape
    share = columns // fsdp
    last = experts - keep
    hbm = pl.BlockSpec(memory_space=pl.ANY)
    return pl.pallas_call(
        functools.partial(ship_kernel, (ep, fsdp), keep),
        in_specs=[hbm] * 5,
        out_specs=[hbm, hbm, hbm],
        out_shape=[
            jax.ShapeDtypeStruct((fsdp, keep, 3, share, rows), jnp.bfloat16),
            jax.ShapeDtypeStruct((fsdp, last, 3, share, rows), jnp.bfloat16),
            jax.ShapeDtypeStruct((ep, router.shape[0], fsdp * router.shape[1]), jnp.bfloat16),
        ],
        scratch_shapes=[
            pltpu.VMEM((2, columns, rows), jnp.float32),
            pltpu.VMEM((2, rows, columns), jnp.float32),
            pltpu.VMEM((2, rows, columns), jnp.float32),
            pltpu.VMEM((RING, fsdp, 3, share, rows), jnp.bfloat16),
            pltpu.VMEM(router.shape, jnp.float32),
            pltpu.VMEM(gain.shape, jnp.float32),
            pltpu.VMEM((router.shape[0], fsdp * router.shape[1]), jnp.bfloat16),
            pltpu.SemaphoreType.DMA((2, 3)),
            pltpu.SemaphoreType.DMA((RING,)),
            pltpu.SemaphoreType.DMA((keep,)),
            pltpu.SemaphoreType.DMA((fsdp,)),
            pltpu.SemaphoreType.DMA((7,)),
        ],
        compiler_params=pltpu.CompilerParams(
            collective_id=0, has_side_effects=True, vmem_limit_bytes=VMEM_LIMIT
        ),
        cost_estimate=pl.CostEstimate(
            flops=experts * rows * columns * 30, bytes_accessed=experts * rows * columns * 18, transcendentals=0
        ),
    )(down, gate, up, router, gain)


def rescale(blocks, width, ready):
    peers, share, inner = blocks.shape
    columns = []
    for r in range(0, share, TILE):
        rows = slice(r, min(r + TILE, share))
        parts = [blocks[p, rows].astype(jnp.float32) for p in range(peers)]
        total = sum(jnp.abs(part) for part in parts)
        scale = jnp.sum(total, axis=1, keepdims=True) / width
        inverse = 1.0 / scale
        for p, part in enumerate(parts):
            ready[rows, p * inner : (p + 1) * inner] = (part * inverse).astype(jnp.bfloat16)
        columns.append(scale)
    column = jnp.concatenate(columns, axis=0)
    return jnp.broadcast_to(column, (share, 128)).T[0:1]


def finish_kernel(x_ref, copies_ref, *refs):
    readies, scales, router_ref = refs[:3], refs[3:6], refs[6]
    held, ready, router, load_sem, store_sem, router_sem = refs[7:]
    peers, count, _, share, inner = x_ref.shape

    def load(e, kind):
        slot = lax.rem(e, DEPTH)
        return pltpu.make_async_copy(x_ref.at[:, e, kind], held.at[slot, kind], load_sem.at[slot, kind])

    def store(e, kind):
        slot = lax.rem(e, DEPTH)
        return pltpu.make_async_copy(ready.at[slot, kind], readies[kind].at[e], store_sem.at[slot, kind])

    for e in range(min(DEPTH, count)):
        for kind in range(3):
            load(e, kind).start()
    enter = pltpu.make_async_copy(copies_ref, router, router_sem.at[0])
    leave = pltpu.make_async_copy(router, router_ref, router_sem.at[1])
    enter.start()

    def step_of(e, carry):
        slot = lax.rem(e, DEPTH)
        for kind in range(3):
            load(e, kind).wait()

            @pl.when(e >= DEPTH)
            def _():
                store(e - DEPTH, kind).wait()

            line = rescale(held.at[slot, kind], peers * inner, ready.at[slot, kind])
            scales[kind][pl.ds(e, 1), :] = line
            store(e, kind).start()

            @pl.when(e + DEPTH < count)
            def _():
                load(e + DEPTH, kind).start()

        return carry

    lax.fori_loop(0, count, step_of, 0)
    enter.wait()
    leave.start()

    def settle(e, carry):
        for kind in range(3):
            store(e, kind).wait()
        return carry

    lax.fori_loop(max(count - DEPTH, 0), count, settle, 0)
    leave.wait()


def finish(received, copies, experts):
    peers, count, _, share, inner = received.shape
    width = peers * inner
    hbm = pl.BlockSpec(memory_space=pl.ANY)
    vmem = pl.BlockSpec(memory_space=pltpu.VMEM)
    return pl.pallas_call(
        finish_kernel,
        in_specs=[hbm, hbm],
        out_specs=[hbm] * 3 + [vmem] * 3 + [hbm],
        out_shape=[jax.ShapeDtypeStruct((experts, share, width), jnp.bfloat16)] * 3
        + [jax.ShapeDtypeStruct((experts, share), jnp.float32)] * 3
        + [jax.ShapeDtypeStruct(copies.shape, jnp.bfloat16)],
        scratch_shapes=[
            pltpu.VMEM((DEPTH, 3, peers, share, inner), jnp.bfloat16),
            pltpu.VMEM((DEPTH, 3, share, width), jnp.bfloat16),
            pltpu.VMEM(copies.shape, jnp.bfloat16),
            pltpu.SemaphoreType.DMA((DEPTH, 3)),
            pltpu.SemaphoreType.DMA((DEPTH, 3)),
            pltpu.SemaphoreType.DMA((2,)),
        ],
        compiler_params=pltpu.CompilerParams(vmem_limit_bytes=VMEM_LIMIT),
        cost_estimate=pl.CostEstimate(
            flops=count * share * width * 12, bytes_accessed=count * share * width * 12, transcendentals=0
        ),
    )(received, copies)


def close_kernel(first, x_ref, *refs):
    readies, scales = refs[6:9], refs[9:12]
    ready, held, load_sem, store_sem = refs[12:]
    peers, count, _, share, inner = x_ref.shape
    loads = [pltpu.make_async_copy(scales[kind], held.at[kind], load_sem.at[kind]) for kind in range(3)]
    for load in loads:
        load.start()
    stores = []

    def store(src, dst):
        stores.append(pltpu.make_async_copy(src, dst, store_sem.at[len(stores)]))
        stores[-1].start()

    for kind in range(3):
        for e in range(count):
            line = rescale(x_ref.at[:, e, kind], peers * inner, ready.at[e, kind])
            store(ready.at[e, kind], readies[kind].at[first + e])
            if e == 0:
                loads[kind].wait()
            held[kind, first + e : first + e + 1, :] = line
        store(held.at[kind], scales[kind])
    for each in stores:
        each.wait()


def close(received, first, carried):
    peers, count, _, share, inner = received.shape
    width = peers * inner
    hbm = pl.BlockSpec(memory_space=pl.ANY)
    vmem = pl.BlockSpec(memory_space=pltpu.VMEM)
    return pl.pallas_call(
        functools.partial(close_kernel, first),
        in_specs=[vmem] + [hbm] * 6,
        out_specs=[hbm] * 6,
        out_shape=[jax.ShapeDtypeStruct(old.shape, old.dtype) for old in carried],
        input_output_aliases={at + 1: at for at in range(6)},
        scratch_shapes=[
            pltpu.VMEM((count, 3, share, width), jnp.bfloat16),
            pltpu.VMEM((3,) + carried[3].shape, jnp.float32),
            pltpu.SemaphoreType.DMA((3,)),
            pltpu.SemaphoreType.DMA((3 * count + 3,)),
        ],
        compiler_params=pltpu.CompilerParams(vmem_limit_bytes=FINISH_LIMIT),
        cost_estimate=pl.CostEstimate(
            flops=count * share * width * 12, bytes_accessed=count * share * width * 12, transcendentals=0
        ),
    )(received, *carried)


def shards(ep, fsdp, train_gate, train_up, train_down, router_weight, router_gain):
    experts = train_gate.shape[0]
    last = max(experts // 16, 1)
    keep = experts - last
    received, packed, copies = ship(
        ep, fsdp, keep, train_down, train_gate, train_up, router_weight.T, router_gain[None]
    )
    rest = lax.all_to_all(packed, "fsdp", split_axis=0, concat_axis=0, tiled=True)
    *done, copies = finish(received, copies, experts)
    ready_down, ready_gate, ready_up, scale_down, scale_gate, scale_up = close(rest, keep, done)
    serve_router = copies.reshape(-1, copies.shape[2]).T
    return (
        jnp.swapaxes(ready_gate, 1, 2),
        jnp.swapaxes(ready_up, 1, 2),
        ready_down,
        scale_gate,
        scale_up,
        scale_down,
        serve_router,
    )


def solution(mesh):
    in_specs = (
        P("ep", "fsdp", None),
        P("ep", "fsdp", None),
        P("ep", None, "fsdp"),
        P("fsdp", "ep"),
        P("fsdp"),
    )
    out_specs = (
        P("ep", None, "fsdp"),
        P("ep", None, "fsdp"),
        P("ep", "fsdp", None),
        P("ep", "fsdp"),
        P("ep", "fsdp"),
        P("ep", "fsdp"),
        P(),
    )
    body = functools.partial(shards, mesh.shape["ep"], mesh.shape["fsdp"])
    return jax.shard_map(body, mesh=mesh, in_specs=in_specs, out_specs=out_specs, check_vma=False)
```

time: 395 us -> 389 us (0.985)
  Pallas kernels: 385 us -> 379 us
    pallas_call x1, Pallas kernels: 361 us -> 355 us  [ship(): pl.pallas_call(functools.partial(ship_kernel, (ep, fsdp), keep), in_specs...]
where the time goes in v2:
time: 389 us
  Pallas kernels  379 us (97%)
  waiting for transfers between devices  4.89 us (1%)
  starting transfers between devices  4.23 us (1%)
    pallas_call x1, Pallas kernels, ship(): pl.pallas_call(functools.partial(ship_kernel, (ep, fsdp), keep), in_specs...  355 us
    pallas_call x1, Pallas kernels, finish(): pl.pallas_call(finish_kernel, in_specs=[hbm, hbm], out_specs=[hbm] * 3 +...  22.4 us
  transfers between devices with their start and end apart: 1, of which 1 were waited for; matrix products, arithmetic and copies ran while one was open for 0% of the time, Pallas kernels for 6%

profile of v2, /device:TPU:0, one launch (start us, length us, event | category | flops | bytes accessed | tf_op | source)
XLA Modules:
  0.0 389.1 jit_solution(18107046252625308363)
XLA Ops:
  0.6 354.6 %shard_map.108 = (bf16[8,15,3,176,256]{4,3,2,1,0:T(8,128)(2,1)}, bf16[8,1,3,176,256]{4,3,2,1,0:T(8,128)(2,1)}, bf16[4,16,2048]{2,1,0:T(8,128)(2,1)}) custom-call(f32[16,1408,256]{2,1,0:T(8,128)} %down_ref.1, f32[16,256,1408]{2,1,0:T(8,128)} %gate_ref.1, f32[16,256,1408]{2,1,0:T(8,128)} %up_ref.1, f32[16,256]{1,0:T(8,128)} %bitcast.9, f32[1,256]{1,0:T(1,128)} %bitcast.10), custom_call_target="tpu_custom_call" | custom-call | flops 173015040 | bytes 103809024 | tf_op jit(solution)/shard_map/pallas_call | solution.py:187
  355.2 4.2 %all-to-all-start = ((bf16[8,1,3,176,256]{4,3,2,1,0:T(8,128)(2,1)}), bf16[8,1,3,176,256]{4,3,2,1,0:T(8,128)(2,1)S(1)}, u32[]{:S(2)}, u32[]{:S(2)}) async-start(bf16[8,1,3,176,256]{4,3,2,1,0:T(8,128)(2,1)} %get-tuple-element.23), calls=%async_computation | async-start | bytes 4325376 | tf_op jit(solution)/shard_map/all_to_all | solution.py:370
  359.4 22.4 %shard_map.109 = (bf16[16,176,2048]{2,1,0:T(8,128)(2,1)}, bf16[16,176,2048]{2,1,0:T(8,128)(2,1)}, bf16[16,176,2048]{2,1,0:T(8,128)(2,1)}, f32[16,176]{1,0:T(8,12...) custom-call(bf16[8,15,3,176,256]{4,3,2,1,0:T(8,128)(2,1)} %get-tuple-element.24.x_ref, ...), custom_call_target="tpu_custom_call" | custom-call | flops 64880640 | bytes 64880640 | tf_op jit(solution)/shard_map/pallas_call | solution.py:292
  381.9 4.9 %all-to-all-done.x_ref = bf16[8,1,3,176,256]{4,3,2,1,0:T(8,128)(2,1)S(1)} async-done(((bf16[8,1,3,176,256]{4,3,2,1,0:T(8,128)(2,1)}), bf16[8,1,3,176,256]{4,3,2,1,0:T(8,128)(2,1)S(1)}, u32[]{:S(2)}, u32[]{:S(2)}) %all-to-all-start) | async-done | bytes 2162720 | tf_op jit(solution)/shard_map/all_to_all | solution.py:370
  386.8 2.3 shard_map.110
Async XLA Ops:
  355.2 31.5 %all-to-all-start = ((bf16[8,1,3,176,256]{4,3,2,1,0:T(8,128)(2,1)}), bf16[8,1,3,176,256]{4,3,2,1,0:T(8,128)(2,1)S(1)}, u32[]{:S(2)}, u32[]{:S(2)}) async-start(bf16[8,1,3,176,256]{4,3,2,1,0:T(8,128)(2,1)} %get-tuple-element.23), calls=%async_computation | async-start | bytes 4325376 | tf_op jit(solution)/shard_map/all_to_all | solution.py:370
